TPU v7x, 32 devices: a whole 2x2x4 slice. The times are simulated.
32 devices in a mesh: grp: 4 (over y, x), row: 8 (over z, core).
Axes of the slice: x: 2, y: 2, z: 4, core: 2. Of those that a mesh axis runs over, the one named last changes fastest.
Arguments:
- blocks: bfloat16 [32, 4, 10, 256, 256], P(('grp', 'row')), may hold values from 0 to 1
- columns: int32 [32, 4, 10], P(('grp', 'row')), may hold values from -1 to 31, as said below
- factor: bfloat16 [64, 8192], P(None, ('grp', 'row')), may hold values from 0 to 0.3, as said below
Outputs:
- updated: float32 [64, 8192], P(None, ('grp', 'row'))
Inputs may be any that keep to these rules, and one draw needn't show every extreme that they name: Tile row i lies in group g = i // 8. In block h of tile row i the live slots come first and name distinct tile columns of group h (h * 8 to h * 8 + 7), none above i; block g always names i itself; blocks h > g are empty; a block holds at most 10 live slots, and -1 marks an empty slot. `factor`: entries are nonnegative.
All inputs are finite; a program needn't handle non-finite values.
Results may differ from a plain program's by a relative error of at most 0.0003.
Values may be sent and summed in bfloat16 or wider, within the bound.
No kernel may reach another device: no remote copies, remote signals or barrier semaphores. Data moves between devices by JAX's collectives and lax.ppermute only.
A program may use at most 128 MiB of HBM per device.

v0:
```python
import jax
import jax.numpy as jnp
from jax import lax
from jax.sharding import PartitionSpec as P

floor_value = 1e-06


def sweep(current, products, gram):

    def update(column, current):
        weights = lax.dynamic_index_in_dim(gram, column, 1, keepdims=False)
        fitted = jnp.dot(weights, current, precision=lax.Precision.HIGHEST)
        target = lax.dynamic_index_in_dim(products, column, 0, keepdims=False)
        present = lax.dynamic_index_in_dim(current, column, 0, keepdims=False)
        diagonal = gram[column, column]
        fresh = jnp.maximum(present + (target - fitted) / diagonal, floor_value)
        return lax.dynamic_update_index_in_dim(current, fresh, column, 0)

    return lax.fori_loop(0, current.shape[0], update, current)


def choose_rows(group_cols, group_number, rows_grp):
    offsets = group_cols - group_number * rows_grp
    positions = lax.broadcasted_iota(jnp.int32, (group_cols.shape[0], rows_grp), 1)
    return (offsets[:, None] == positions) & (group_cols >= 0)[:, None]


def lower_work(group_tiles, group_cols, group_number, group_factor, rows_grp):
    rank_count, span = group_factor.shape
    tile_size = span // rows_grp
    stacked = group_factor.reshape(rank_count, rows_grp, tile_size)
    selected = choose_rows(group_cols, group_number, rows_grp)
    fetched = jnp.einsum(
        "sn,rnt->srt", selected.astype(jnp.bfloat16), stacked, preferred_element_type=jnp.float32
    ).astype(jnp.bfloat16)
    return jnp.einsum("srv,suv->ru", fetched, group_tiles, preferred_element_type=jnp.float32)


def per_device(blocks, columns, factor):
    tiles_dev = blocks[0]
    cols_dev = columns[0]
    rank_count, tile_size = factor.shape
    rows_grp = lax.axis_size("row")
    group_count = lax.axis_size("grp")
    span = rows_grp * tile_size
    gram = lax.psum(jnp.dot(factor, factor.T, preferred_element_type=jnp.float32), ("grp", "row"))
    group_factor = lax.all_gather(factor, "row", axis=1, tiled=True)
    my_group = lax.axis_index("grp")
    slot_count = cols_dev.shape[1]
    live = (cols_dev >= 0).astype(jnp.float32)
    mirror = jnp.einsum("ru,hsuv->hsrv", factor, tiles_dev, preferred_element_type=jnp.float32)
    mirror = mirror * live[:, :, None, None]
    arrived, arrived_cols = (
        lax.all_to_all(mirror, "grp", split_axis=0, concat_axis=0, tiled=True),
        lax.all_to_all(cols_dev, "grp", split_axis=0, concat_axis=0, tiled=True),
    )
    flat_cols = arrived_cols.reshape(group_count * slot_count)
    selected = choose_rows(flat_cols, my_group, rows_grp).astype(jnp.float32)
    flat_mirror = arrived.reshape(group_count * slot_count, rank_count, tile_size)
    spread = jnp.einsum("sn,srv->rnv", selected, flat_mirror, precision=lax.Precision.HIGHEST)
    mirror_sum = lax.psum_scatter(
        spread.reshape(rank_count, span), "row", scatter_dimension=1, tiled=True
    )
    lower_sum = jnp.zeros((rank_count, tile_size), jnp.float32)
    piece = lax.all_gather(group_factor, "grp", axis=1, tiled=True)
    begin_at = jnp.int32(0)
    for offset in range(piece.shape[1] // span):
        group_number = begin_at // span + offset
        group_tiles = lax.dynamic_index_in_dim(tiles_dev, group_number, 0, keepdims=False)
        group_cols = lax.dynamic_index_in_dim(cols_dev, group_number, 0, keepdims=False)
        block_cols = lax.dynamic_slice_in_dim(piece, offset * span, span, 1)
        lower_sum = lower_sum + lower_work(
            group_tiles, group_cols, group_number, block_cols, rows_grp
        )
    products = lower_sum + mirror_sum
    return sweep(factor.astype(jnp.float32), products, gram)


def solution(mesh):
    in_specs = (
        P(("grp", "row"), None, None, None, None),
        P(("grp", "row"), None, None),
        P(None, ("grp", "row")),
    )
    out_specs = P(None, ("grp", "row"))
    return jax.shard_map(
        per_device, mesh=mesh, in_specs=in_specs, out_specs=out_specs, check_vma=False
    )
```

profile of v0, /device:TPU:0, one launch (start us, length us, event | category | flops | bytes accessed | tf_op | source)
XLA Modules:
  0.0 246.8 jit_solution(16195418602525848965)
XLA Ops:
  7.4 5.2 %all-to-all-start.1 = ((s32[4,1,10]{2,1,0:T(1,128)}), s32[4,1,10]{2,1,0:T(1,128)S(1)}, u32[]{:S(2)}, u32[]{:S(2)}) async-start(s32[4,1,10]{2,1,0:T(1,128)} %bitcast.144), calls=%async_computation.1 | async-start | bytes 4096 | tf_op jit(solution)/shard_map/all_to_all | solution.py:56
  12.6 15.7 %all_gather.6 = bf16[64,2048]{1,0:T(8,128)(2,1)} all-gather(bf16[64,256]{1,0:T(8,128)(2,1)} %param.7), channel_id=1, replica_groups=mesh['grp'=4,'row'=8] {'row'}, dimensions={1}, use_global_device_ids=true | all-gather | bytes 294912 | tf_op jit(solution)/shard_map/all_gather | solution.py:48
  28.3 0.7 convert_bitcast_fusion
  29.0 5.1 %multiply_bitcast_fusion = f32[4,10,64,256]{3,2,1,0:T(8,128)} fusion(bf16[1,4,10,256,256]{4,3,2,1,0:T(8,128)(2,1)} %param.5, f32[4,10]{1,0:T(4,128)S(1)} %convert_bitcast_fusion, bf16[64,256]{1,0:T(8,128)(2,1)} %param.7), kind=kOutput, calls=%fused_computation.10 | convolution fusion | flops 336199680 | bytes 7897248 | tf_op jit(solution)/shard_map/ru,hsuv->hsrv/dot_general | solution.py:52
  34.1 4.4 %all-to-all-start = ((f32[4,10,64,256]{3,2,1,0:T(8,128)}), f32[4,10,64,256]{3,2,1,0:T(8,128)S(1)}, u32[]{:S(2)}, u32[]{:S(2)}) async-start(f32[4,10,64,256]{3,2,1,0:T(8,128)} %multiply_bitcast_fusion), calls=%async_computation | async-start | bytes 5242880 | tf_op jit(solution)/shard_map/all_to_all | solution.py:55
  38.6 71.8 %psum.7 = f32[64,64]{1,0:T(8,128)S(1)} all-reduce(f32[64,64]{1,0:T(8,128)S(1)} %fusion.75), channel_id=1, replica_groups=mesh['grp'=4,'row'=8] {'grp','row'}, use_global_device_ids=true, to_apply=%region_0.0 | all-reduce | flops 4096 | bytes 32768 | tf_op jit(solution)/shard_map/psum | solution.py:47
  110.8 1.3 fusion.74
  112.2 1.2 convolution_convert_fusion.3
  113.3 1.1 convolution_convert_fusion.2
  114.5 2.4 fusion.4
  116.9 1.0 copy.21
  117.9 2.0 fusion.20
  120.7 1.8 fusion.41
  122.5 1.8 fusion.38
  124.4 24.2 %reduce-scatter.2.cloned.1.call-done = f32[64,256]{1,0:T(8,128)} async-done(((f32[64,2048]{1,0:T(8,128)}), f32[64,256]{1,0:T(8,128)}) %reduce-scatter.2.cloned.1.call-update) | async-done | bytes 65552 | tf_op jit(solution)/shard_map/reduce_scatter | solution.py:62
  148.6 1.8 fusion.35
  150.4 88.3 %while.13 = (s32[]{:T(128)}, f32[64,256]{1,0:T(8,128)S(1)}, f32[64,256]{1,0:T(8,128)S(1)}, f32[64,64]{0,1:T(8,128)S(1)}, s32[]{:T(128)}, /*index=5*/s32[]{:T(128)}) while((s32[]{:T(128)}, f32[64,256]{1,0:T(8,128)S(1)}, f32[64,256]{1,0:T(8,128)S(1)}, f32[64,64]{0,1:T(8,128)S(1)}, s32[]{:T(128)}, /*index=5*/s32[]{:T(128)}) %tuple.42), condition=%wide.region_3.4_spmd, body=%wide.region_2.3_spmd.sunk | while | flops 197634 | bytes 77417 | solution.py:20
  150.6 0.6 dynamic_slice.138
  151.9 0.6 dynamic_slice.138
  153.3 0.6 dynamic_slice.138
  154.7 0.6 dynamic_slice.138
  156.1 0.6 dynamic_slice.138
  157.5 0.6 dynamic_slice.138
  158.8 0.6 dynamic_slice.138
  160.2 0.6 dynamic_slice.138
  161.6 0.6 dynamic_slice.138
  163.0 0.6 dynamic_slice.138
  164.4 0.6 dynamic_slice.138
  165.7 0.6 dynamic_slice.138
  167.1 0.6 dynamic_slice.138
  168.5 0.6 dynamic_slice.138
  169.9 0.6 dynamic_slice.138
  171.3 0.6 dynamic_slice.138
  172.6 0.6 dynamic_slice.138
  174.0 0.6 dynamic_slice.138
  175.4 0.6 dynamic_slice.138
  176.8 0.6 dynamic_slice.138
  178.2 0.6 dynamic_slice.138
  179.5 0.6 dynamic_slice.138
  180.9 0.6 dynamic_slice.138
  182.3 0.6 dynamic_slice.138
  183.7 0.6 dynamic_slice.138
  185.1 0.6 dynamic_slice.138
  186.4 0.6 dynamic_slice.138
  187.8 0.6 dynamic_slice.138
  189.2 0.6 dynamic_slice.138
  190.6 0.6 dynamic_slice.138
  238.7 0.6 copy-done
  (320 shorter events, 69.9 us)
Async XLA Ops:
  7.4 26.7 %all-to-all-start.1 = ((s32[4,1,10]{2,1,0:T(1,128)}), s32[4,1,10]{2,1,0:T(1,128)S(1)}, u32[]{:S(2)}, u32[]{:S(2)}) async-start(s32[4,1,10]{2,1,0:T(1,128)} %bitcast.144), calls=%async_computation.1 | async-start | bytes 4096 | tf_op jit(solution)/shard_map/all_to_all | solution.py:56
  12.6 98.2 %all-gather.2.cloned.1.call-start = ((), (), s32[]{:S(2)}) async-start(), calls=%async_computation.3 | async-start | bytes 1310720 | tf_op jit(solution)/shard_map/all_gather | solution.py:66
  34.0 4.4 %copy-start.1 = (bf16[64,256]{1,0:T(8,128)(2,1)S(1)}, bf16[64,256]{1,0:T(8,128)(2,1)}, u32[]{:S(2)}) copy-start(bf16[64,256]{1,0:T(8,128)(2,1)} %param.7) | copy-start | bytes 98308
  34.0 76.4 %copy-start.3 = (s32[1,4,10]{2,1,0:T(4,128)S(1)}, s32[1,4,10]{2,1,0:T(4,128)}, u32[]{:S(2)}) copy-start(s32[1,4,10]{2,1,0:T(4,128)} %param.6) | copy-start | bytes 484
  34.1 80.4 %all-to-all-start = ((f32[4,10,64,256]{3,2,1,0:T(8,128)}), f32[4,10,64,256]{3,2,1,0:T(8,128)S(1)}, u32[]{:S(2)}, u32[]{:S(2)}) async-start(f32[4,10,64,256]{3,2,1,0:T(8,128)} %multiply_bitcast_fusion), calls=%async_computation | async-start | bytes 5242880 | tf_op jit(solution)/shard_map/all_to_all | solution.py:55
  38.4 110.1 %reduce-scatter.2.cloned.1.call-start = ((), (), s32[]{:S(2)}) async-start(), calls=%async_computation.4 | async-start | bytes 589824 | tf_op jit(solution)/shard_map/reduce_scatter | solution.py:62
  117.8 2.9 %copy-start.2 = (bf16[10,64,256]{2,0,1:T(8,128)(2,1)S(1)}, bf16[10,64,256]{2,0,1:T(8,128)(2,1)}, u32[]{:S(2)}) copy-start(bf16[10,64,256]{2,0,1:T(8,128)(2,1)} %convolution_convert_fusion.2) | copy-start | bytes 983044
  238.7 0.6 copy-start
Sparse Core Ops, SparseCore 0:
  28.4 48.7 all-gather.1
Sparse Core Ops, SparseCore 1:
  117.9 30.6 reduce-scatter.1
where the time goes:
time: 248 us; the launch traced here: 247 us
  blocking collectives  87.5 us (35%)
  local copies, waits for them, and re-layouts  44.1 us (18%)
  other arithmetic  36.8 us (15%)
  matrix products  27.2 us (11%)
  waiting for transfers between devices  24.2 us (10%)
  between operations  15 us (6%)
  starting transfers between devices  9.57 us (4%)
    psum x1, blocking collectives, per_device(): lax.psum(jnp.dot(factor, factor.T, preferred_element_type=jnp.float32), (...  71.8 us
    dynamic_slice x64, local copies, waits for them, and re-layouts, update(): diagonal = gram[column, column]  37.4 us
    max x64, other arithmetic, update(): fresh = jnp.maximum(present + (target - fitted) / diagonal, floor_value)  36.1 us
    reduce_scatter x1, waiting for transfers between devices, per_device(): lax.psum_scatter(spread.reshape(rank_count, span), 'row', scatter_dimensi...  24.2 us
    all_gather x1, blocking collectives, per_device(): group_factor = lax.all_gather(factor, 'row', axis=1, tiled=True)  15.7 us
    dot_general x64, matrix products, update(): fitted = jnp.dot(weights, current, precision=lax.Precision.HIGHEST)  9.16 us
    dot_general x4, matrix products, lower_work(): jnp.einsum('srv,suv->ru', fetched, group_tiles, preferred_element_type=jn...  7.5 us
    all_to_all x1, starting transfers between devices, per_device(): lax.all_to_all(cols_dev, 'grp', split_axis=0, concat_axis=0, tiled=True)  5.19 us
  transfers between devices with their start and end apart: 4, of which 1 were waited for; matrix products, arithmetic and copies ran while one was open for 7% of the time, Pallas kernels for 0%

commit v1 on v0

--- a/solution.py
+++ b/solution.py
@@ -44,7 +44,9 @@
     rows_grp = lax.axis_size("row")
     group_count = lax.axis_size("grp")
     span = rows_grp * tile_size
-    gram = lax.psum(jnp.dot(factor, factor.T, preferred_element_type=jnp.float32), ("grp", "row"))
+    part = jnp.dot(factor, factor.T, preferred_element_type=jnp.float32)
+    pieces = lax.all_gather(part, ("grp", "row"), axis=0, tiled=False)
+    gram = pieces.sum(axis=0)
     group_factor = lax.all_gather(factor, "row", axis=1, tiled=True)
     my_group = lax.axis_index("grp")
     slot_count = cols_dev.shape[1]

time: 248 us -> 224 us (0.903)
  blocking collectives: 87.5 us -> 65.4 us
  waiting for transfers between devices: 24.2 us -> 21 us
    psum x1 -> x0, blocking collectives: 71.8 us -> none  [per_device(): lax.psum(jnp.dot(factor, factor.T, preferred_element_type=jnp.float32), (...]
    all_gather x0 -> x1, blocking collectives: none -> 49.7 us  [per_device(): pieces = lax.all_gather(part, ('grp', 'row'), axis=0, tiled=False)]
    reduce_scatter x1, waiting for transfers between devices: 24.2 us -> 21 us  [per_device(): lax.psum_scatter(spread.reshape(rank_count, span), 'row', scatter_dimensi...]
  transfers between devices with their start and end apart: 4 -> 4, of which waited for: 1 -> 1; matrix products, arithmetic and copies ran while one was open for 7% -> 8% of each run, Pallas kernels for 0% -> 0%
where the time goes in v1:
time: 224 us; the launch traced here: 223 us
  blocking collectives  65.4 us (29%)
  local copies, waits for them, and re-layouts  44.1 us (20%)
  other arithmetic  38.1 us (17%)
  matrix products  27.2 us (12%)
  waiting for transfers between devices  21 us (9%)
  between operations  15 us (7%)
  starting transfers between devices  9.57 us (4%)
  loops' own time  2.29 us (1%)
    all_gather x1, blocking collectives, per_device(): pieces = lax.all_gather(part, ('grp', 'row'), axis=0, tiled=False)  49.7 us
    dynamic_slice x64, local copies, waits for them, and re-layouts, update(): diagonal = gram[column, column]  37.4 us
    max x64, other arithmetic, update(): fresh = jnp.maximum(present + (target - fitted) / diagonal, floor_value)  36.1 us
    reduce_scatter x1, waiting for transfers between devices, per_device(): lax.psum_scatter(spread.reshape(rank_count, span), 'row', scatter_dimensi...  21 us
    all_gather x1, blocking collectives, per_device(): group_factor = lax.all_gather(factor, 'row', axis=1, tiled=True)  15.7 us
    dot_general x64, matrix products, update(): fitted = jnp.dot(weights, current, precision=lax.Precision.HIGHEST)  9.16 us
    dot_general x4, matrix products, lower_work(): jnp.einsum('srv,suv->ru', fetched, group_tiles, preferred_element_type=jn...  7.48 us
    all_to_all x1, starting transfers between devices, per_device(): lax.all_to_all(cols_dev, 'grp', split_axis=0, concat_axis=0, tiled=True)  5.19 us
  transfers between devices with their start and end apart: 4, of which 1 were waited for; matrix products, arithmetic and copies ran while one was open for 8% of the time, Pallas kernels for 0%

profile of v1, /device:TPU:0, one launch (start us, length us, event | category | flops | bytes accessed | tf_op | source)
XLA Modules:
  0.0 222.7 jit_solution(15885760792799633113)
XLA Ops:
  7.4 5.2 %all-to-all-start.1 = ((s32[4,1,10]{2,1,0:T(1,128)}), s32[4,1,10]{2,1,0:T(1,128)S(1)}, u32[]{:S(2)}, u32[]{:S(2)}) async-start(s32[4,1,10]{2,1,0:T(1,128)} %bitcast.146), calls=%async_computation.1 | async-start | bytes 4096 | tf_op jit(solution)/shard_map/all_to_all | solution.py:58
  12.6 15.7 %all_gather.12 = bf16[64,2048]{1,0:T(8,128)(2,1)} all-gather(bf16[64,256]{1,0:T(8,128)(2,1)} %param.7), channel_id=1, replica_groups=mesh['grp'=4,'row'=8] {'row'}, dimensions={1}, use_global_device_ids=true | all-gather | bytes 294912 | tf_op jit(solution)/shard_map/all_gather | solution.py:50
  28.3 0.7 convert_bitcast_fusion
  29.0 5.1 %multiply_bitcast_fusion = f32[4,10,64,256]{3,2,1,0:T(8,128)} fusion(bf16[1,4,10,256,256]{4,3,2,1,0:T(8,128)(2,1)} %param.5, f32[4,10]{1,0:T(4,128)S(1)} %convert_bitcast_fusion, bf16[64,256]{1,0:T(8,128)(2,1)} %param.7), kind=kOutput, calls=%fused_computation.10 | convolution fusion | flops 336199680 | bytes 7897248 | tf_op jit(solution)/shard_map/ru,hsuv->hsrv/dot_general | solution.py:54
  34.2 4.4 %all-to-all-start = ((f32[4,10,64,256]{3,2,1,0:T(8,128)}), f32[4,10,64,256]{3,2,1,0:T(8,128)S(1)}, u32[]{:S(2)}, u32[]{:S(2)}) async-start(f32[4,10,64,256]{3,2,1,0:T(8,128)} %multiply_bitcast_fusion), calls=%async_computation | async-start | bytes 5242880 | tf_op jit(solution)/shard_map/all_to_all | solution.py:57
  38.6 49.7 %all-gather = f32[2048,64]{1,0:T(8,128)} all-gather(f32[64,64]{1,0:T(8,128)S(1)} %fusion.75), channel_id=2, replica_groups=mesh['grp'=4,'row'=8] {'grp','row'}, dimensions={0}, use_global_device_ids=true | all-gather | bytes 540672 | tf_op jit(solution)/shard_map/all_gather | solution.py:48
  88.2 1.3 reduce_sum.9
  89.9 1.3 fusion.74
  91.3 1.2 convolution_convert_fusion.3
  92.5 1.1 convolution_convert_fusion.2
  93.6 2.4 %fusion.4 = f32[64,256,8]{1,2,0:T(8,128)S(1)} fusion(f32[40,64,256]{2,1,0:T(8,128)S(1)} %bitcast.130, s32[40]{0:T(128)S(1)} %sub.63, pred[40]{0:T(512)(128)(4,1)S(1)} %ge.72), kind=kOutput, calls=%fused_computation.8 | convolution fusion | flops 62915200 | bytes 3145928 | tf_op jit(solution)/shard_map/sn,srv->rnv/dot_general | solution.py:63
  96.0 1.0 copy.20
  97.0 2.0 fusion.20
  99.9 1.8 fusion.41
  101.7 1.8 fusion.38
  103.5 21.0 %reduce-scatter.2.cloned.1.call-done = f32[64,256]{1,0:T(8,128)} async-done(((f32[64,2048]{1,0:T(8,128)}), f32[64,256]{1,0:T(8,128)}) %reduce-scatter.2.cloned.1.call-update) | async-done | bytes 65552 | tf_op jit(solution)/shard_map/reduce_scatter | solution.py:64
  124.5 1.8 fusion.35
  126.3 88.3 %while.13 = (s32[]{:T(128)}, f32[64,256]{1,0:T(8,128)S(1)}, f32[64,256]{1,0:T(8,128)S(1)}, f32[64,64]{0,1:T(8,128)S(1)}, s32[]{:T(128)}, /*index=5*/s32[]{:T(128)}) while((s32[]{:T(128)}, f32[64,256]{1,0:T(8,128)S(1)}, f32[64,256]{1,0:T(8,128)S(1)}, f32[64,64]{0,1:T(8,128)S(1)}, s32[]{:T(128)}, /*index=5*/s32[]{:T(128)}) %tuple.41), condition=%wide.region_3.4_spmd, body=%wide.region_2.3_spmd.sunk | while | flops 197634 | bytes 77417 | solution.py:20
  126.5 0.6 dynamic_slice.138
  127.9 0.6 dynamic_slice.138
  129.2 0.6 dynamic_slice.138
  130.6 0.6 dynamic_slice.138
  132.0 0.6 dynamic_slice.138
  133.4 0.6 dynamic_slice.138
  134.8 0.6 dynamic_slice.138
  136.1 0.6 dynamic_slice.138
  137.5 0.6 dynamic_slice.138
  138.9 0.6 dynamic_slice.138
  140.3 0.6 dynamic_slice.138
  141.7 0.6 dynamic_slice.138
  143.0 0.6 dynamic_slice.138
  144.4 0.6 dynamic_slice.138
  145.8 0.6 dynamic_slice.138
  147.2 0.6 dynamic_slice.138
  148.6 0.6 dynamic_slice.138
  149.9 0.6 dynamic_slice.138
  151.3 0.6 dynamic_slice.138
  152.7 0.6 dynamic_slice.138
  154.1 0.6 dynamic_slice.138
  155.5 0.6 dynamic_slice.138
  156.8 0.6 dynamic_slice.138
  158.2 0.6 dynamic_slice.138
  159.6 0.6 dynamic_slice.138
  161.0 0.6 dynamic_slice.138
  162.4 0.6 dynamic_slice.138
  163.7 0.6 dynamic_slice.138
  165.1 0.6 dynamic_slice.138
  214.6 0.6 copy-done
  (321 shorter events, 70.5 us)
Async XLA Ops:
  7.4 26.8 %all-to-all-start.1 = ((s32[4,1,10]{2,1,0:T(1,128)}), s32[4,1,10]{2,1,0:T(1,128)S(1)}, u32[]{:S(2)}, u32[]{:S(2)}) async-start(s32[4,1,10]{2,1,0:T(1,128)} %bitcast.146), calls=%async_computation.1 | async-start | bytes 4096 | tf_op jit(solution)/shard_map/all_to_all | solution.py:58
  12.6 77.3 %all-gather.3.cloned.1.call-start = ((), (), s32[]{:S(2)}) async-start(), calls=%async_computation.3 | async-start | bytes 1310720 | tf_op jit(solution)/shard_map/all_gather | solution.py:68
  29.0 5.1 %copy-start.1 = (bf16[64,256]{1,0:T(8,128)(2,1)S(1)}, bf16[64,256]{1,0:T(8,128)(2,1)}, u32[]{:S(2)}) copy-start(bf16[64,256]{1,0:T(8,128)(2,1)} %param.7) | copy-start | bytes 98308
  34.2 55.5 %copy-start.3 = (s32[1,4,10]{2,1,0:T(4,128)S(1)}, s32[1,4,10]{2,1,0:T(4,128)}, u32[]{:S(2)}) copy-start(s32[1,4,10]{2,1,0:T(4,128)} %param.6) | copy-start | bytes 484
  34.2 59.4 %all-to-all-start = ((f32[4,10,64,256]{3,2,1,0:T(8,128)}), f32[4,10,64,256]{3,2,1,0:T(8,128)S(1)}, u32[]{:S(2)}, u32[]{:S(2)}) async-start(f32[4,10,64,256]{3,2,1,0:T(8,128)} %multiply_bitcast_fusion), calls=%async_computation | async-start | bytes 5242880 | tf_op jit(solution)/shard_map/all_to_all | solution.py:57
  38.6 85.9 %reduce-scatter.2.cloned.1.call-start = ((), (), s32[]{:S(2)}) async-start(), calls=%async_computation.4 | async-start | bytes 589824 | tf_op jit(solution)/shard_map/reduce_scatter | solution.py:64
  97.0 2.9 %copy-start.2 = (bf16[10,64,256]{2,0,1:T(8,128)(2,1)S(1)}, bf16[10,64,256]{2,0,1:T(8,128)(2,1)}, u32[]{:S(2)}) copy-start(bf16[10,64,256]{2,0,1:T(8,128)(2,1)} %convolution_convert_fusion.2) | copy-start | bytes 983044
  214.6 0.6 copy-start
Sparse Core Ops, SparseCore 0:
  28.4 51.0 all-gather.2
Sparse Core Ops, SparseCore 1:
  97.1 27.4 reduce-scatter.1
